TPU v7x, 512 devices: a whole 4x8x8 slice. The times are simulated.
512 devices in a mesh: ty: 32 (over y, x_hi, core), tx: 16 (over z, x_lo).
Axes of the slice: x: 4 (x_hi: 2, x_lo: 2; x = x_hi * 2 + x_lo), y: 8, z: 8, core: 2. Of those that a mesh axis runs over, the one named last changes fastest.
Arguments:
- noise: float32 [4096, 4096], P('ty', 'tx'), may hold values from -6 to 6
- root_spectrum: float32 [384, 512], replicated, may hold values from 0.25 to 4
Outputs:
- field: float32 [4096, 4096], P('ty', 'tx')
All inputs are finite; a program needn't handle non-finite values.
Results may differ from a plain program's by a relative error of at most 0.0003.
Values sent between devices are 32-bit elements; how exact they have to be, the bound alone decides.
A program may use at most 64 MiB of HBM per device.

v0:
```python
import functools
import math

import jax
import jax.numpy as jnp
import numpy as np
from jax import lax
from jax.experimental import pallas as pl
from jax.experimental.pallas import tpu as pltpu
from jax.sharding import PartitionSpec as P

MARGIN = 128
EY = 384
EX = 512
BLOCK = 256
HALF_Y = EY // 2
HALF_X = EX // 2
MESH = pl.DeviceIdType.MESH


def split_table(table):
    high = table.astype(jnp.bfloat16)
    low = (table - high.astype(np.float64)).astype(jnp.bfloat16)
    return np.stack([high, low])


def row_basis():
    ky = np.arange(HALF_Y)[:, None]
    y = np.arange(EY)[None, :]
    angle = 2.0 * math.pi * (ky * y % EY) / EY
    lower = -np.sin(angle)
    lower[0] = np.cos(math.pi * np.arange(EY))
    return np.concatenate([np.cos(angle), lower])


def column_basis():
    x = np.arange(HALF_X)[:, None]
    bases = []
    for odd in (0, 1):
        kx = 2 * np.arange(HALF_X // 2)[None, :] + odd
        angle = 2.0 * math.pi * (kx * x % EX) / EX
        sine = np.sin(angle)
        if not odd:
            sine[:, 0] = np.cos(math.pi * np.arange(HALF_X))
        bases.append(np.concatenate([np.cos(angle), sine], axis=1))
    return np.stack(bases)


def row_weights():
    knots = (np.arange(EY) + 0.5) / MARGIN
    return np.where(
        knots < 1.0,
        0.5 * knots * knots,
        np.where(
            knots < 2.0,
            0.5 * (-2.0 * knots * knots + 6.0 * knots - 3.0),
            0.5 * (3.0 - knots) * (3.0 - knots),
        ),
    )


def tables():
    rows = row_basis()
    forward = split_table(rows)
    forward = forward.reshape(2, EY, 3, MARGIN).transpose(2, 0, 1, 3)
    back = split_table((rows * row_weights()[None, :]).T)
    back = back.reshape(2, 3, MARGIN, EY).transpose(1, 0, 2, 3)
    columns = split_table(column_basis())
    return np.ascontiguousarray(forward), np.ascontiguousarray(back), columns


def split(value):
    high = value.astype(jnp.bfloat16)
    return high, (value - high.astype(jnp.float32)).astype(jnp.bfloat16)


def dot(left, right):
    return jnp.dot(left, right, preferred_element_type=jnp.float32)


def dot_t(left, right):
    return lax.dot_general(left, right, (((1,), (1,)), ((), ())), preferred_element_type=jnp.float32)


def three(product, left, right):
    return product(left[0], right[0]) + product(left[0], right[1]) + product(left[1], right[0])


def iota(shape, dim):
    return lax.broadcasted_iota(jnp.int32, shape, dim)


def indicator(condition):
    return jnp.where(condition, 1.0, 0.0)


def spectrum_terms(spectrum, even_ref, cross_ref):
    source = iota((EX, 128), 0)
    lane = iota((EX, 128), 1)
    folds = []
    for sign in (1.0, -1.0):
        for odd in (0, 1):
            kx = 2 * lane + odd
            fold = indicator(source == kx) + sign * indicator(source == EX - kx)
            if sign < 0 and not odd:
                fold = jnp.where(lane == 0, indicator(source == HALF_X), fold)
            folds.append(fold)
    fold = jnp.concatenate(folds, axis=1).astype(jnp.bfloat16)
    high, low = split(spectrum * (1.0 / (EY * EX)))
    folded = dot(high, fold) + dot(low, fold)
    high, low = split(folded)
    ky = iota((HALF_Y, EY), 0)
    row = iota((HALF_Y, EY), 1)
    straight = indicator(row == ky)
    mirrored = indicator(row == EY - ky)
    sums = (straight + mirrored).astype(jnp.bfloat16)
    gaps = jnp.where(ky == 0, 0.0, straight - mirrored).astype(jnp.bfloat16)
    even = dot(sums, high[:, :384]) + dot(sums, low[:, :384])
    cross = dot(gaps, high[:, 256:]) + dot(gaps, low[:, 256:])
    first_row = iota((HALF_Y, 128), 0) == 0
    first_lane = iota((HALF_Y, 128), 1) == 0
    middle = folded[HALF_Y : HALF_Y + 1]
    for slot, group in ((0, 0), (1, 0), (2, 1), (3, 1)):
        upper = even[:, 128 * group : 128 * group + 128]
        edge = jnp.broadcast_to(middle[:, 128 * group : 128 * group + 128], (HALF_Y, 128))
        if slot == 1:
            upper = jnp.where(first_lane, even[:, 256:384], upper)
            edge = jnp.where(first_lane, jnp.broadcast_to(middle[:, 256:384], (HALF_Y, 128)), edge)
        even_ref[0:HALF_Y, pl.ds(128 * slot, 128)] = upper
        even_ref[HALF_Y:EY, pl.ds(128 * slot, 128)] = jnp.where(first_row, edge, upper)
    cross_ref[:, 0:128] = jnp.where(first_lane, 0.0, cross[:, :128])
    cross_ref[:, 128:256] = cross[:, 128:]


def kernel(
    n_ty,
    n_tx,
    noise_ref,
    spectrum_ref,
    forward_ref,
    back_ref,
    columns_ref,
    out_ref,
    window,
    spectrum,
    forward,
    back,
    columns,
    even,
    cross,
    staged,
    blended,
    side,
    from_remote,
    from_sibling,
    from_side,
    from_corner,
    local_sem,
    send_sem,
    recv_sem,
):
    me_y = lax.axis_index("ty")
    me_x = lax.axis_index("tx")
    core = lax.rem(me_y, 2)
    sibling_y = me_y + 1 - 2 * core
    remote_y = lax.rem(me_y + 2 * core - 1 + n_ty, n_ty)
    left_x = lax.rem(me_x + n_tx - 1, n_tx)
    right_x = lax.rem(me_x + 1, n_tx)

    sibling = (sibling_y, me_x)
    remote = (remote_y, me_x)
    left = (me_y, left_x)
    right = (me_y, right_x)
    corner_left = (remote_y, left_x)
    corner_right = (remote_y, right_x)
    partners = (remote, corner_left, corner_right, left, right, sibling)

    barrier = pltpu.get_barrier_semaphore()
    for partner in partners:
        pl.semaphore_signal(barrier, inc=1, device_id=partner, device_id_type=MESH)

    def local(source, target, index):
        copy = pltpu.make_async_copy(source, target, local_sem.at[index])
        copy.start()
        return copy

    own = window.at[1, :, pl.ds(MARGIN, BLOCK)]
    load_noise = local(noise_ref, own, 0)
    load_spectrum = local(spectrum_ref, spectrum, 1)
    slots = (2 * core, 1, 2 - 2 * core)
    load_tables = [local(forward_ref.at[slots[i]], forward.at[i], 2 + i) for i in range(3)]
    load_columns = local(columns_ref, columns, 5)
    load_back = [local(back_ref.at[slots[i]], back.at[i], 6 + i) for i in range(3)]

    load_noise.wait()
    pl.semaphore_wait(barrier, len(partners))

    def send(source, target, index, device):
        copy = pltpu.make_async_remote_copy(
            src_ref=source,
            dst_ref=target,
            send_sem=send_sem.at[index],
            recv_sem=recv_sem.at[index],
            device_id=device,
            device_id_type=MESH,
        )
        copy.start()
        return copy

    left_strip = pl.ds(0, MARGIN)
    left_half = pl.ds(MARGIN, MARGIN)
    right_half = pl.ds(2 * MARGIN, MARGIN)
    right_strip = pl.ds(3 * MARGIN, MARGIN)
    centre = pl.ds(MARGIN, BLOCK)

    to_right = send(window.at[1, :, right_half], window.at[1, :, left_strip], 0, right)
    to_left = send(window.at[1, :, left_half], window.at[1, :, right_strip], 1, left)
    to_remote = send(own, window.at[0, :, centre], 2, remote)
    to_corner_right = send(window.at[1, :, right_half], window.at[0, :, left_strip], 3, corner_right)
    to_corner_left = send(window.at[1, :, left_half], window.at[0, :, right_strip], 4, corner_left)
    to_sibling = send(own, window.at[2, :, centre], 5, sibling)

    load_spectrum.wait()
    spectrum_terms(spectrum[...], even, cross)
    for load in load_tables:
        load.wait()
    load_columns.wait()

    to_right.wait_recv()
    pass_left = send(window.at[1, :, left_strip], window.at[2, :, left_strip], 6, sibling)
    to_left.wait_recv()
    pass_right = send(window.at[1, :, right_strip], window.at[2, :, right_strip], 7, sibling)
    to_sibling.wait_recv()
    pass_left.wait_recv()
    pass_right.wait_recv()

    near = split(window[1:3].reshape(2 * MARGIN, EX))
    near_tables = [jnp.concatenate([forward[1, i], forward[2, i]], axis=1) for i in range(2)]
    staged[...] = three(dot, near_tables, near)
    to_remote.wait_recv()
    to_corner_right.wait_recv()
    to_corner_left.wait_recv()
    far = split(window[0])
    rows = staged[...] + three(dot, (forward[0, 0], forward[0, 1]), far)

    halves = []
    for parity in range(2):
        lower, upper = rows[:, :HALF_X], rows[:, HALF_X:]
        folded = lower + upper if parity == 0 else lower - upper
        waves = three(dot, split(folded), (columns[0, parity], columns[1, parity]))
        mixed = cross[:, pl.ds(128 * parity, 128)]
        scale = even[:, pl.ds(256 * parity, 256)]
        flat = waves * scale
        real_c, real_s = waves[:HALF_Y, :128], waves[:HALF_Y, 128:]
        imag_c, imag_s = waves[HALF_Y:, :128], waves[HALF_Y:, 128:]
        shift = jnp.concatenate(
            [
                jnp.concatenate([mixed * imag_s, -(mixed * imag_c)], axis=1),
                jnp.concatenate([-(mixed * real_s), mixed * real_c], axis=1),
            ],
            axis=0,
        )
        halves.append(three(dot_t, split(flat + shift), (columns[0, parity], columns[1, parity])))
    position = iota((1, HALF_X), 1).astype(jnp.float32) + 0.5
    rising = position * (1.0 / HALF_X)
    falling = 1.0 - rising
    strips = jnp.concatenate(
        [(halves[0] + halves[1]) * rising, (halves[0] - halves[1]) * falling], axis=1
    )
    strips = split(strips)

    for load in load_back:
        load.wait()
    blended[0] = three(dot, (back[0, 0], back[0, 1]), strips)
    add_remote = send(blended.at[0, :, centre], from_remote, 8, remote)
    add_corner_left = send(blended.at[0, :, left_strip], from_corner.at[1], 9, corner_left)
    add_corner_right = send(blended.at[0, :, right_strip], from_corner.at[0], 10, corner_right)
    blended[2] = three(dot, (back[2, 0], back[2, 1]), strips)
    add_sibling = send(blended.at[2], from_sibling, 11, sibling)
    blended[1] = three(dot, (back[1, 0], back[1, 1]), strips)
    add_sibling.wait_recv()
    side[0] = blended[1, :, left_strip] + from_sibling[:, left_strip]
    add_left = send(side.at[0], from_side.at[1], 12, left)
    side[1] = blended[1, :, right_strip] + from_sibling[:, right_strip]
    add_right = send(side.at[1], from_side.at[0], 13, right)
    middle = blended[1, :, centre] + from_sibling[:, centre]
    add_remote.wait_recv()
    middle = middle + from_remote[...]
    add_corner_left.wait_recv()
    add_corner_right.wait_recv()
    corners = jnp.concatenate([from_corner[0], from_corner[1]], axis=1)
    middle = middle + corners
    add_left.wait_recv()
    add_right.wait_recv()
    out_ref[...] = middle + jnp.concatenate([from_side[0], from_side[1]], axis=1)
    for copy in (
        to_right,
        to_left,
        to_remote,
        to_corner_right,
        to_corner_left,
        to_sibling,
        pass_left,
        pass_right,
        add_remote,
        add_corner_left,
        add_corner_right,
        add_sibling,
        add_left,
        add_right,
    ):
        copy.wait_send()


def per_device(n_ty, n_tx, noise, root_spectrum):
    forward, back, columns = tables()
    anywhere = pl.BlockSpec(memory_space=pl.ANY)
    f32 = jnp.float32
    bf16 = jnp.bfloat16
    return pl.pallas_call(
        functools.partial(kernel, n_ty, n_tx),
        out_shape=jax.ShapeDtypeStruct(noise.shape, f32),
        in_specs=[anywhere] * 5,
        out_specs=pl.BlockSpec(memory_space=pltpu.VMEM),
        scratch_shapes=[
            pltpu.VMEM((3, MARGIN, EX), f32),
            pltpu.VMEM((EY, EX), f32),
            pltpu.VMEM((3, 2, EY, MARGIN), bf16),
            pltpu.VMEM((3, 2, MARGIN, EY), bf16),
            pltpu.VMEM((2, 2, HALF_X, HALF_X), bf16),
            pltpu.VMEM((EY, EX), f32),
            pltpu.VMEM((HALF_Y, HALF_X), f32),
            pltpu.VMEM((EY, EX), f32),
            pltpu.VMEM((3, MARGIN, EX), f32),
            pltpu.VMEM((2, MARGIN, MARGIN), f32),
            pltpu.VMEM((MARGIN, BLOCK), f32),
            pltpu.VMEM((MARGIN, EX), f32),
            pltpu.VMEM((2, MARGIN, MARGIN), f32),
            pltpu.VMEM((2, MARGIN, MARGIN), f32),
            pltpu.SemaphoreType.DMA((9,)),
            pltpu.SemaphoreType.DMA((14,)),
            pltpu.SemaphoreType.DMA((14,)),
        ],
        compiler_params=pltpu.CompilerParams(collective_id=0, has_side_effects=True),
        name="field_tile",
    )(noise, root_spectrum, jnp.asarray(forward), jnp.asarray(back), jnp.asarray(columns))


def solution(mesh):
    placed = (P("ty", "tx"), P())
    body = functools.partial(per_device, mesh.shape["ty"], mesh.shape["tx"])
    return jax.shard_map(
        body, mesh=mesh, in_specs=placed, out_specs=P("ty", "tx"), check_vma=False
    )
```

profile of v0, /device:TPU:1, one launch (start us, length us, event | category | flops | bytes accessed | tf_op | source)
XLA Modules:
  0.0 33.3 jit_solution(8853466384352612044)
XLA Ops:
  0.0 31.7 %field_tile.1 = f32[128,256]{1,0:T(8,128)} custom-call(f32[128,256]{1,0:T(8,128)} %noise_ref.1, f32[384,512]{1,0:T(8,128)} %spectrum_ref.1, bf16[3,2,384,128]{3,2,1,0:T(8,128)(2,1)} %constant.6.clone.forward_ref, bf16[3,2,128,384]{3,2,1,0:T(8,128)(2,1)} %constant.7.clone.back_ref, bf16[2,2,256,256]{3,2,1,0:T(8,128)(2,1)} %constant.8.clone.columns_ref), custom_call_target="tpu_custom_call" | custom-call | tf_op jit(solution)/shard_map/field_tile/pallas_call | solution.py:320
  31.7 1.6 %copy.7 = f32[128,256]{1,0:T(8,128)} copy(f32[128,256]{1,0:T(8,128)} %field_tile.1) | data formatting | bytes 262144
where the time goes:
time: 33.4 us; the launch traced here: 33.3 us
  Pallas kernels  31.7 us (95%)
  local copies, waits for them, and re-layouts  1.57 us (5%)
    pallas_call x1, Pallas kernels, per_device(): pl.pallas_call(functools.partial(kernel, n_ty, n_tx), out_shape=jax.Shape...  31.7 us
    unnamed x1, local copies, waits for them, and re-layouts  1.57 us

commit v1 on v0

--- a/solution.py
+++ b/solution.py
@@ -94,7 +94,7 @@
     return jnp.where(condition, 1.0, 0.0)
 
 
-def spectrum_terms(spectrum, even_ref, cross_ref):
+def fold_columns(spectrum):
     source = iota((EX, 128), 0)
     lane = iota((EX, 128), 1)
     folds = []
@@ -107,7 +107,10 @@
             folds.append(fold)
     fold = jnp.concatenate(folds, axis=1).astype(jnp.bfloat16)
     high, low = split(spectrum * (1.0 / (EY * EX)))
-    folded = dot(high, fold) + dot(low, fold)
+    return dot(high, fold) + dot(low, fold)
+
+
+def fold_rows(folded, even_ref, cross_ref):
     high, low = split(folded)
     ky = iota((HALF_Y, EY), 0)
     row = iota((HALF_Y, EY), 1)
@@ -193,6 +196,9 @@
     load_back = [local(back_ref.at[slots[i]], back.at[i], 6 + i) for i in range(3)]
 
     load_noise.wait()
+    load_spectrum.wait()
+    folded = fold_columns(spectrum[...])
+    spectrum[...] = folded
     pl.semaphore_wait(barrier, len(partners))
 
     def send(source, target, index, device):
@@ -220,39 +226,55 @@
     to_corner_left = send(window.at[1, :, left_half], window.at[0, :, right_strip], 4, corner_left)
     to_sibling = send(own, window.at[2, :, centre], 5, sibling)
 
-    load_spectrum.wait()
-    spectrum_terms(spectrum[...], even, cross)
+    fold_rows(spectrum[...], even, cross)
     for load in load_tables:
         load.wait()
     load_columns.wait()
+
+    def to_waves(rows):
+        lower, upper = rows[:, :HALF_X], rows[:, HALF_X:]
+        return jnp.concatenate(
+            [
+                three(dot, split(lower + upper), (columns[0, 0], columns[1, 0])),
+                three(dot, split(lower - upper), (columns[0, 1], columns[1, 1])),
+            ],
+            axis=1,
+        )
+
+    position = iota((1, HALF_X), 1).astype(jnp.float32) + 0.5
+    rising = position * (1.0 / HALF_X)
+    falling = 1.0 - rising
+
+    def from_waves(waves):
+        straight = three(dot_t, split(waves[:, :HALF_X]), (columns[0, 0], columns[1, 0]))
+        turned = three(dot_t, split(waves[:, HALF_X:]), (columns[0, 1], columns[1, 1]))
+        return (straight + turned) * rising, (straight - turned) * falling
 
     to_right.wait_recv()
     pass_left = send(window.at[1, :, left_strip], window.at[2, :, left_strip], 6, sibling)
     to_left.wait_recv()
     pass_right = send(window.at[1, :, right_strip], window.at[2, :, right_strip], 7, sibling)
+    own_waves = split(to_waves(window[1]))
+    staged[...] = three(dot, (forward[1, 0], forward[1, 1]), own_waves)
     to_sibling.wait_recv()
     pass_left.wait_recv()
     pass_right.wait_recv()
-
-    near = split(window[1:3].reshape(2 * MARGIN, EX))
-    near_tables = [jnp.concatenate([forward[1, i], forward[2, i]], axis=1) for i in range(2)]
-    staged[...] = three(dot, near_tables, near)
+    sibling_waves = split(to_waves(window[2]))
+    staged[...] += three(dot, (forward[2, 0], forward[2, 1]), sibling_waves)
+    for load in load_back:
+        load.wait()
     to_remote.wait_recv()
     to_corner_right.wait_recv()
     to_corner_left.wait_recv()
-    far = split(window[0])
-    rows = staged[...] + three(dot, (forward[0, 0], forward[0, 1]), far)
+    remote_waves = split(to_waves(window[0]))
+    waves = staged[...] + three(dot, (forward[0, 0], forward[0, 1]), remote_waves)
 
     halves = []
     for parity in range(2):
-        lower, upper = rows[:, :HALF_X], rows[:, HALF_X:]
-        folded = lower + upper if parity == 0 else lower - upper
-        waves = three(dot, split(folded), (columns[0, parity], columns[1, parity]))
+        part = waves[:, 256 * parity : 256 * parity + 256]
         mixed = cross[:, pl.ds(128 * parity, 128)]
-        scale = even[:, pl.ds(256 * parity, 256)]
-        flat = waves * scale
-        real_c, real_s = waves[:HALF_Y, :128], waves[:HALF_Y, 128:]
-        imag_c, imag_s = waves[HALF_Y:, :128], waves[HALF_Y:, 128:]
+        real_c, real_s = part[:HALF_Y, :128], part[:HALF_Y, 128:]
+        imag_c, imag_s = part[HALF_Y:, :128], part[HALF_Y:, 128:]
         shift = jnp.concatenate(
             [
                 jnp.concatenate([mixed * imag_s, -(mixed * imag_c)], axis=1),
@@ -260,36 +282,32 @@
             ],
             axis=0,
         )
-        halves.append(three(dot_t, split(flat + shift), (columns[0, parity], columns[1, parity])))
-    position = iota((1, HALF_X), 1).astype(jnp.float32) + 0.5
-    rising = position * (1.0 / HALF_X)
-    falling = 1.0 - rising
-    strips = jnp.concatenate(
-        [(halves[0] + halves[1]) * rising, (halves[0] - halves[1]) * falling], axis=1
-    )
-    strips = split(strips)
-
-    for load in load_back:
-        load.wait()
-    blended[0] = three(dot, (back[0, 0], back[0, 1]), strips)
+        halves.append(part * even[:, pl.ds(256 * parity, 256)] + shift)
+    product = split(jnp.concatenate(halves, axis=1))
+
+    def rows_of(slot):
+        return three(dot, (back[slot, 0], back[slot, 1]), product)
+
+    low_half, high_half = pl.ds(0, HALF_X), pl.ds(HALF_X, HALF_X)
+    blended[2] = rows_of(2)
+    add_sibling = send(blended.at[2], from_sibling, 11, sibling)
+    blended[0, :, low_half], blended[0, :, high_half] = from_waves(rows_of(0))
     add_remote = send(blended.at[0, :, centre], from_remote, 8, remote)
     add_corner_left = send(blended.at[0, :, left_strip], from_corner.at[1], 9, corner_left)
     add_corner_right = send(blended.at[0, :, right_strip], from_corner.at[0], 10, corner_right)
-    blended[2] = three(dot, (back[2, 0], back[2, 1]), strips)
-    add_sibling = send(blended.at[2], from_sibling, 11, sibling)
-    blended[1] = three(dot, (back[1, 0], back[1, 1]), strips)
+    blended[1] = rows_of(1)
     add_sibling.wait_recv()
-    side[0] = blended[1, :, left_strip] + from_sibling[:, left_strip]
+    low, high = from_waves(blended[1] + from_sibling[...])
+    side[0] = low[:, :MARGIN]
     add_left = send(side.at[0], from_side.at[1], 12, left)
-    side[1] = blended[1, :, right_strip] + from_sibling[:, right_strip]
+    side[1] = high[:, MARGIN:]
     add_right = send(side.at[1], from_side.at[0], 13, right)
-    middle = blended[1, :, centre] + from_sibling[:, centre]
+    middle = jnp.concatenate([low[:, MARGIN:], high[:, :MARGIN]], axis=1)
     add_remote.wait_recv()
     middle = middle + from_remote[...]
     add_corner_left.wait_recv()
     add_corner_right.wait_recv()
-    corners = jnp.concatenate([from_corner[0], from_corner[1]], axis=1)
-    middle = middle + corners
+    middle = middle + jnp.concatenate([from_corner[0], from_corner[1]], axis=1)
     add_left.wait_recv()
     add_right.wait_recv()
     out_ref[...] = middle + jnp.concatenate([from_side[0], from_side[1]], axis=1)
@@ -319,7 +337,7 @@
     bf16 = jnp.bfloat16
     return pl.pallas_call(
         functools.partial(kernel, n_ty, n_tx),
-        out_shape=jax.ShapeDtypeStruct(noise.shape, f32),
+        out_shape=pltpu.VMEM(noise.shape, f32),
         in_specs=[anywhere] * 5,
         out_specs=pl.BlockSpec(memory_space=pltpu.VMEM),
         scratch_shapes=[

time: 33.4 us -> 31 us (0.928)
  Pallas kernels: 31.7 us -> 30.2 us
  local copies, waits for them, and re-layouts: 1.57 us -> 0.66 us
    pallas_call x1, Pallas kernels: 31.7 us -> 30.2 us  [per_device(): pl.pallas_call(functools.partial(kernel, n_ty, n_tx), out_shape=pltpu.VME...]
    unnamed x1, local copies, waits for them, and re-layouts: 1.57 us -> 0.66 us
where the time goes in v1:
time: 31 us; the launch traced here: 30.9 us
  Pallas kernels  30.2 us (97%)
  local copies, waits for them, and re-layouts  0.66 us (2%)
    pallas_call x1, Pallas kernels, per_device(): pl.pallas_call(functools.partial(kernel, n_ty, n_tx), out_shape=pltpu.VME...  30.2 us
    unnamed x1, local copies, waits for them, and re-layouts  0.66 us

profile of v1, /device:TPU:1, one launch (start us, length us, event | category | flops | bytes accessed | tf_op | source)
XLA Modules:
  0.0 30.9 jit_solution(8997832722525393133)
XLA Ops:
  0.0 30.2 %field_tile.1 = f32[128,256]{1,0:T(8,128)S(1)} custom-call(f32[128,256]{1,0:T(8,128)} %noise_ref.1, f32[384,512]{1,0:T(8,128)} %spectrum_ref.1, bf16[3,2,384,128]{3,2,1,0:T(8,128)(2,1)} %constant.6.clone.forward_ref, bf16[3,2,128,384]{3,2,1,0:T(8,128)(2,1)} %constant.7.clone.back_ref, bf16[2,2,256,256]{3,2,1,0:T(8,128)(2,1)} %constant.8.clone.columns_ref), custom_call_target="tpu_custom_call" | custom-call | tf_op jit(solution)/shard_map/field_tile/pallas_call | solution.py:338
  30.2 0.7 %copy.7 = f32[128,256]{1,0:T(8,128)} copy(f32[128,256]{1,0:T(8,128)S(1)} %field_tile.1) | data formatting | bytes 262144

commit v2 on v1

--- a/solution.py
+++ b/solution.py
@@ -83,7 +83,12 @@
 
 
 def three(product, left, right):
-    return product(left[0], right[0]) + product(left[0], right[1]) + product(left[1], right[0])
+    if product is dot_t:
+        return dot_t(jnp.concatenate([left[0], left[1], left[0]], axis=1), jnp.concatenate([right[0], right[0], right[1]], axis=1))
+    return dot(
+        jnp.concatenate([left[0], left[0], left[1]], axis=1),
+        jnp.concatenate([right[0], right[1], right[0]], axis=0),
+    )
 
 
 def iota(shape, dim):

time: 31 us -> 30.7 us (level)
  no operation moved by 1% of the time
where the time goes in v2:
time: 30.7 us; the launch traced here: 30.6 us
  Pallas kernels  29.9 us (97%)
  local copies, waits for them, and re-layouts  0.66 us (2%)
    pallas_call x1, Pallas kernels, per_device(): pl.pallas_call(functools.partial(kernel, n_ty, n_tx), out_shape=pltpu.VME...  29.9 us
    unnamed x1, local copies, waits for them, and re-layouts  0.66 us

profile of v2, /device:TPU:1, one launch (start us, length us, event | category | flops | bytes accessed | tf_op | source)
XLA Modules:
  0.0 30.6 jit_solution(8592901558204115000)
XLA Ops:
  0.0 29.9 %field_tile.1 = f32[128,256]{1,0:T(8,128)S(1)} custom-call(f32[128,256]{1,0:T(8,128)} %noise_ref.1, f32[384,512]{1,0:T(8,128)} %spectrum_ref.1, bf16[3,2,384,128]{3,2,1,0:T(8,128)(2,1)} %constant.6.clone.forward_ref, bf16[3,2,128,384]{3,2,1,0:T(8,128)(2,1)} %constant.7.clone.back_ref, bf16[2,2,256,256]{3,2,1,0:T(8,128)(2,1)} %constant.8.clone.columns_ref), custom_call_target="tpu_custom_call" | custom-call | tf_op jit(solution)/shard_map/field_tile/pallas_call | solution.py:343
  29.9 0.7 %copy.7 = f32[128,256]{1,0:T(8,128)} copy(f32[128,256]{1,0:T(8,128)S(1)} %field_tile.1) | data formatting | bytes 262144

commit v3 on v2

--- a/solution.py
+++ b/solution.py
@@ -66,7 +66,8 @@
     back = split_table((rows * row_weights()[None, :]).T)
     back = back.reshape(2, 3, MARGIN, EY).transpose(1, 0, 2, 3)
     columns = split_table(column_basis())
-    return np.ascontiguousarray(forward), np.ascontiguousarray(back), columns
+    turned = columns.transpose(0, 1, 3, 2)
+    return [np.ascontiguousarray(table) for table in (forward, back, columns, turned)]
 
 
 def split(value):
@@ -78,13 +79,7 @@
     return jnp.dot(left, right, preferred_element_type=jnp.float32)
 
 
-def dot_t(left, right):
-    return lax.dot_general(left, right, (((1,), (1,)), ((), ())), preferred_element_type=jnp.float32)
-
-
-def three(product, left, right):
-    if product is dot_t:
-        return dot_t(jnp.concatenate([left[0], left[1], left[0]], axis=1), jnp.concatenate([right[0], right[0], right[1]], axis=1))
+def three(left, right):
     return dot(
         jnp.concatenate([left[0], left[0], left[1]], axis=1),
         jnp.concatenate([right[0], right[1], right[0]], axis=0),
@@ -148,12 +143,14 @@
     forward_ref,
     back_ref,
     columns_ref,
+    turned_ref,
     out_ref,
     window,
     spectrum,
     forward,
     back,
     columns,
+    turned,
     even,
     cross,
     staged,
@@ -198,6 +195,7 @@
     slots = (2 * core, 1, 2 - 2 * core)
     load_tables = [local(forward_ref.at[slots[i]], forward.at[i], 2 + i) for i in range(3)]
     load_columns = local(columns_ref, columns, 5)
+    load_turned = local(turned_ref, turned, 9)
     load_back = [local(back_ref.at[slots[i]], back.at[i], 6 + i) for i in range(3)]
 
     load_noise.wait()
@@ -226,9 +224,9 @@
 
     to_right = send(window.at[1, :, right_half], window.at[1, :, left_strip], 0, right)
     to_left = send(window.at[1, :, left_half], window.at[1, :, right_strip], 1, left)
+    to_corner_left = send(window.at[1, :, left_half], window.at[0, :, right_strip], 4, corner_left)
     to_remote = send(own, window.at[0, :, centre], 2, remote)
     to_corner_right = send(window.at[1, :, right_half], window.at[0, :, left_strip], 3, corner_right)
-    to_corner_left = send(window.at[1, :, left_half], window.at[0, :, right_strip], 4, corner_left)
     to_sibling = send(own, window.at[2, :, centre], 5, sibling)
 
     fold_rows(spectrum[...], even, cross)
@@ -240,8 +238,8 @@
         lower, upper = rows[:, :HALF_X], rows[:, HALF_X:]
         return jnp.concatenate(
             [
-                three(dot, split(lower + upper), (columns[0, 0], columns[1, 0])),
-                three(dot, split(lower - upper), (columns[0, 1], columns[1, 1])),
+                three(split(lower + upper), (columns[0, 0], columns[1, 0])),
+                three(split(lower - upper), (columns[0, 1], columns[1, 1])),
             ],
             axis=1,
         )
@@ -251,28 +249,28 @@
     falling = 1.0 - rising
 
     def from_waves(waves):
-        straight = three(dot_t, split(waves[:, :HALF_X]), (columns[0, 0], columns[1, 0]))
-        turned = three(dot_t, split(waves[:, HALF_X:]), (columns[0, 1], columns[1, 1]))
-        return (straight + turned) * rising, (straight - turned) * falling
+        straight = three(split(waves[:, :HALF_X]), (turned[0, 0], turned[1, 0]))
+        crossed = three(split(waves[:, HALF_X:]), (turned[0, 1], turned[1, 1]))
+        return (straight + crossed) * rising, (straight - crossed) * falling
 
     to_right.wait_recv()
     pass_left = send(window.at[1, :, left_strip], window.at[2, :, left_strip], 6, sibling)
     to_left.wait_recv()
     pass_right = send(window.at[1, :, right_strip], window.at[2, :, right_strip], 7, sibling)
     own_waves = split(to_waves(window[1]))
-    staged[...] = three(dot, (forward[1, 0], forward[1, 1]), own_waves)
+    staged[...] = three((forward[1, 0], forward[1, 1]), own_waves)
     to_sibling.wait_recv()
     pass_left.wait_recv()
     pass_right.wait_recv()
     sibling_waves = split(to_waves(window[2]))
-    staged[...] += three(dot, (forward[2, 0], forward[2, 1]), sibling_waves)
-    for load in load_back:
+    staged[...] += three((forward[2, 0], forward[2, 1]), sibling_waves)
+    for load in (*load_back, load_turned):
         load.wait()
     to_remote.wait_recv()
     to_corner_right.wait_recv()
     to_corner_left.wait_recv()
     remote_waves = split(to_waves(window[0]))
-    waves = staged[...] + three(dot, (forward[0, 0], forward[0, 1]), remote_waves)
+    waves = staged[...] + three((forward[0, 0], forward[0, 1]), remote_waves)
 
     halves = []
     for parity in range(2):
@@ -291,7 +289,7 @@
     product = split(jnp.concatenate(halves, axis=1))
 
     def rows_of(slot):
-        return three(dot, (back[slot, 0], back[slot, 1]), product)
+        return three((back[slot, 0], back[slot, 1]), product)
 
     low_half, high_half = pl.ds(0, HALF_X), pl.ds(HALF_X, HALF_X)
     blended[2] = rows_of(2)
@@ -336,20 +334,21 @@
 
 
 def per_device(n_ty, n_tx, noise, root_spectrum):
-    forward, back, columns = tables()
+    constants = [jnp.asarray(table) for table in tables()]
     anywhere = pl.BlockSpec(memory_space=pl.ANY)
     f32 = jnp.float32
     bf16 = jnp.bfloat16
     return pl.pallas_call(
         functools.partial(kernel, n_ty, n_tx),
         out_shape=pltpu.VMEM(noise.shape, f32),
-        in_specs=[anywhere] * 5,
+        in_specs=[anywhere] * 6,
         out_specs=pl.BlockSpec(memory_space=pltpu.VMEM),
         scratch_shapes=[
             pltpu.VMEM((3, MARGIN, EX), f32),
             pltpu.VMEM((EY, EX), f32),
             pltpu.VMEM((3, 2, EY, MARGIN), bf16),
             pltpu.VMEM((3, 2, MARGIN, EY), bf16),
+            pltpu.VMEM((2, 2, HALF_X, HALF_X), bf16),
             pltpu.VMEM((2, 2, HALF_X, HALF_X), bf16),
             pltpu.VMEM((EY, EX), f32),
             pltpu.VMEM((HALF_Y, HALF_X), f32),
@@ -360,13 +359,13 @@
             pltpu.VMEM((MARGIN, EX), f32),
             pltpu.VMEM((2, MARGIN, MARGIN), f32),
             pltpu.VMEM((2, MARGIN, MARGIN), f32),
-            pltpu.SemaphoreType.DMA((9,)),
+            pltpu.SemaphoreType.DMA((10,)),
             pltpu.SemaphoreType.DMA((14,)),
             pltpu.SemaphoreType.DMA((14,)),
         ],
         compiler_params=pltpu.CompilerParams(collective_id=0, has_side_effects=True),
         name="field_tile",
-    )(noise, root_spectrum, jnp.asarray(forward), jnp.asarray(back), jnp.asarray(columns))
+    )(noise, root_spectrum, *constants)
 
 
 def solution(mesh):

time: 30.7 us -> 30.1 us (0.980)
  the two profiles are of different devices: /device:TPU:1 before, /device:TPU:57 now
where the time goes in v3:
time: 30.1 us; the launch traced here: 29.9 us
  Pallas kernels  29.3 us (97%)
  local copies, waits for them, and re-layouts  0.66 us (2%)
    pallas_call x1, Pallas kernels, per_device(): pl.pallas_call(functools.partial(kernel, n_ty, n_tx), out_shape=pltpu.VME...  29.3 us
    unnamed x1, local copies, waits for them, and re-layouts  0.66 us

profile of v3, /device:TPU:57, one launch (start us, length us, event | category | flops | bytes accessed | tf_op | source)
XLA Modules:
  0.0 29.9 jit_solution(2990825468436824738)
XLA Ops:
  0.0 29.3 %field_tile.1 = f32[128,256]{1,0:T(8,128)S(1)} custom-call(f32[128,256]{1,0:T(8,128)} %noise_ref.1, f32[384,512]{1,0:T(8,128)} %spectrum_ref.1, bf16[3,2,384,128]{3,2,1,0:T(8,128)(2,1)} %constant.8.clone.forward_ref, bf16[3,2,128,384]{3,2,1,0:T(8,128)(2,1)} %constant.9.clone.back_ref, bf16[2,2,256,256]{3,2,1,0:T(8,128)(2,1)} %constant.10.clone.columns_ref, ...), custom_call_target="tpu_custom_call" | custom-call | tf_op jit(solution)/shard_map/field_tile/pallas_call | solution.py:341
  29.3 0.7 %copy.8 = f32[128,256]{1,0:T(8,128)} copy(f32[128,256]{1,0:T(8,128)S(1)} %field_tile.1) | data formatting | bytes 262144

commit v4 on v3

--- a/solution.py
+++ b/solution.py
@@ -263,14 +263,17 @@
     pass_left.wait_recv()
     pass_right.wait_recv()
     sibling_waves = split(to_waves(window[2]))
-    staged[...] += three((forward[2, 0], forward[2, 1]), sibling_waves)
     for load in (*load_back, load_turned):
         load.wait()
     to_remote.wait_recv()
     to_corner_right.wait_recv()
     to_corner_left.wait_recv()
     remote_waves = split(to_waves(window[0]))
-    waves = staged[...] + three((forward[0, 0], forward[0, 1]), remote_waves)
+    pairs = ((forward[2, 0], forward[2, 1], sibling_waves), (forward[0, 0], forward[0, 1], remote_waves))
+    waves = staged[...] + dot(
+        jnp.concatenate([t for high, low, _ in pairs for t in (high, high, low)], axis=1),
+        jnp.concatenate([w for _, _, (high, low) in pairs for w in (high, low, high)], axis=0),
+    )
 
     halves = []
     for parity in range(2):
@@ -292,12 +295,12 @@
         return three((back[slot, 0], back[slot, 1]), product)
 
     low_half, high_half = pl.ds(0, HALF_X), pl.ds(HALF_X, HALF_X)
-    blended[2] = rows_of(2)
-    add_sibling = send(blended.at[2], from_sibling, 11, sibling)
     blended[0, :, low_half], blended[0, :, high_half] = from_waves(rows_of(0))
     add_remote = send(blended.at[0, :, centre], from_remote, 8, remote)
     add_corner_left = send(blended.at[0, :, left_strip], from_corner.at[1], 9, corner_left)
     add_corner_right = send(blended.at[0, :, right_strip], from_corner.at[0], 10, corner_right)
+    blended[2] = rows_of(2)
+    add_sibling = send(blended.at[2], from_sibling, 11, sibling)
     blended[1] = rows_of(1)
     add_sibling.wait_recv()
     low, high = from_waves(blended[1] + from_sibling[...])

time: 30.1 us -> 29.8 us (0.990)
  the two profiles are of different devices: /device:TPU:57 before, /device:TPU:1 now
where the time goes in v4:
time: 29.8 us; the launch traced here: 29.7 us
  Pallas kernels  29.1 us (98%)
  local copies, waits for them, and re-layouts  0.66 us (2%)
    pallas_call x1, Pallas kernels, per_device(): pl.pallas_call(functools.partial(kernel, n_ty, n_tx), out_shape=pltpu.VME...  29.1 us
    unnamed x1, local copies, waits for them, and re-layouts  0.66 us

profile of v4, /device:TPU:1, one launch (start us, length us, event | category | flops | bytes accessed | tf_op | source)
XLA Modules:
  0.0 29.7 jit_solution(2192467280675699609)
XLA Ops:
  0.0 29.1 %field_tile.1 = f32[128,256]{1,0:T(8,128)S(1)} custom-call(f32[128,256]{1,0:T(8,128)} %noise_ref.1, f32[384,512]{1,0:T(8,128)} %spectrum_ref.1, bf16[3,2,384,128]{3,2,1,0:T(8,128)(2,1)} %constant.8.clone.forward_ref, bf16[3,2,128,384]{3,2,1,0:T(8,128)(2,1)} %constant.9.clone.back_ref, bf16[2,2,256,256]{3,2,1,0:T(8,128)(2,1)} %constant.10.clone.columns_ref, ...), custom_call_target="tpu_custom_call" | custom-call | tf_op jit(solution)/shard_map/field_tile/pallas_call | solution.py:344
  29.1 0.7 %copy.8 = f32[128,256]{1,0:T(8,128)} copy(f32[128,256]{1,0:T(8,128)S(1)} %field_tile.1) | data formatting | bytes 262144

commit v5 on v4

--- a/solution.py
+++ b/solution.py
@@ -222,12 +222,12 @@
     right_strip = pl.ds(3 * MARGIN, MARGIN)
     centre = pl.ds(MARGIN, BLOCK)
 
-    to_right = send(window.at[1, :, right_half], window.at[1, :, left_strip], 0, right)
+    to_sibling = send(own, window.at[2, :, centre], 5, sibling)
     to_left = send(window.at[1, :, left_half], window.at[1, :, right_strip], 1, left)
     to_corner_left = send(window.at[1, :, left_half], window.at[0, :, right_strip], 4, corner_left)
+    to_right = send(window.at[1, :, right_half], window.at[1, :, left_strip], 0, right)
     to_remote = send(own, window.at[0, :, centre], 2, remote)
     to_corner_right = send(window.at[1, :, right_half], window.at[0, :, left_strip], 3, corner_right)
-    to_sibling = send(own, window.at[2, :, centre], 5, sibling)
 
     fold_rows(spectrum[...], even, cross)
     for load in load_tables:
@@ -297,10 +297,10 @@
     low_half, high_half = pl.ds(0, HALF_X), pl.ds(HALF_X, HALF_X)
     blended[0, :, low_half], blended[0, :, high_half] = from_waves(rows_of(0))
     add_remote = send(blended.at[0, :, centre], from_remote, 8, remote)
+    blended[2] = rows_of(2)
+    add_sibling = send(blended.at[2], from_sibling, 11, sibling)
     add_corner_left = send(blended.at[0, :, left_strip], from_corner.at[1], 9, corner_left)
     add_corner_right = send(blended.at[0, :, right_strip], from_corner.at[0], 10, corner_right)
-    blended[2] = rows_of(2)
-    add_sibling = send(blended.at[2], from_sibling, 11, sibling)
     blended[1] = rows_of(1)
     add_sibling.wait_recv()
     low, high = from_waves(blended[1] + from_sibling[...])

time: 29.8 us -> 29.8 us (level)
  no operation moved by 1% of the time
where the time goes in v5:
time: 29.8 us; the launch traced here: 29.7 us
  Pallas kernels  29 us (97%)
  local copies, waits for them, and re-layouts  0.66 us (2%)
    pallas_call x1, Pallas kernels, per_device(): pl.pallas_call(functools.partial(kernel, n_ty, n_tx), out_shape=pltpu.VME...  29 us
    unnamed x1, local copies, waits for them, and re-layouts  0.66 us

profile of v5, /device:TPU:1, one launch (start us, length us, event | category | flops | bytes accessed | tf_op | source)
XLA Modules:
  0.0 29.7 jit_solution(13578589489195629055)
XLA Ops:
  0.0 29.0 %field_tile.1 = f32[128,256]{1,0:T(8,128)S(1)} custom-call(f32[128,256]{1,0:T(8,128)} %noise_ref.1, f32[384,512]{1,0:T(8,128)} %spectrum_ref.1, bf16[3,2,384,128]{3,2,1,0:T(8,128)(2,1)} %constant.8.clone.forward_ref, bf16[3,2,128,384]{3,2,1,0:T(8,128)(2,1)} %constant.9.clone.back_ref, bf16[2,2,256,256]{3,2,1,0:T(8,128)(2,1)} %constant.10.clone.columns_ref, ...), custom_call_target="tpu_custom_call" | custom-call | tf_op jit(solution)/shard_map/field_tile/pallas_call | solution.py:344
  29.1 0.7 %copy.8 = f32[128,256]{1,0:T(8,128)} copy(f32[128,256]{1,0:T(8,128)S(1)} %field_tile.1) | data formatting | bytes 262144

commit v6 on v5

--- a/solution.py
+++ b/solution.py
@@ -253,10 +253,10 @@
         crossed = three(split(waves[:, HALF_X:]), (turned[0, 1], turned[1, 1]))
         return (straight + crossed) * rising, (straight - crossed) * falling
 
+    to_left.wait_recv()
+    pass_right = send(window.at[1, :, right_strip], window.at[2, :, right_strip], 7, sibling)
     to_right.wait_recv()
     pass_left = send(window.at[1, :, left_strip], window.at[2, :, left_strip], 6, sibling)
-    to_left.wait_recv()
-    pass_right = send(window.at[1, :, right_strip], window.at[2, :, right_strip], 7, sibling)
     own_waves = split(to_waves(window[1]))
     staged[...] = three((forward[1, 0], forward[1, 1]), own_waves)
     to_sibling.wait_recv()

time: 29.8 us -> 29.8 us (level)
  no operation moved by 1% of the time
where the time goes in v6:
time: 29.8 us; the launch traced here: 29.7 us
  Pallas kernels  29 us (97%)
  local copies, waits for them, and re-layouts  0.66 us (2%)
    pallas_call x1, Pallas kernels, per_device(): pl.pallas_call(functools.partial(kernel, n_ty, n_tx), out_shape=pltpu.VME...  29 us
    unnamed x1, local copies, waits for them, and re-layouts  0.66 us

profile of v6, /device:TPU:1, one launch (start us, length us, event | category | flops | bytes accessed | tf_op | source)
XLA Modules:
  0.0 29.7 jit_solution(10978554522149226246)
XLA Ops:
  0.0 29.0 %field_tile.1 = f32[128,256]{1,0:T(8,128)S(1)} custom-call(f32[128,256]{1,0:T(8,128)} %noise_ref.1, f32[384,512]{1,0:T(8,128)} %spectrum_ref.1, bf16[3,2,384,128]{3,2,1,0:T(8,128)(2,1)} %constant.8.clone.forward_ref, bf16[3,2,128,384]{3,2,1,0:T(8,128)(2,1)} %constant.9.clone.back_ref, bf16[2,2,256,256]{3,2,1,0:T(8,128)(2,1)} %constant.10.clone.columns_ref, ...), custom_call_target="tpu_custom_call" | custom-call | tf_op jit(solution)/shard_map/field_tile/pallas_call | solution.py:344
  29.0 0.7 %copy.8 = f32[128,256]{1,0:T(8,128)} copy(f32[128,256]{1,0:T(8,128)S(1)} %field_tile.1) | data formatting | bytes 262144
